TPU v7x, 32 devices: a whole 2x2x4 slice. The times are simulated.
32 devices in a mesh: dp: 2 (over x), tm: 4 (over z), mp: 4 (over y, core).
Axes of the slice: x: 2, y: 2, z: 4, core: 2. Of those that a mesh axis runs over, the one named last changes fastest.
Arguments:
- features: bfloat16 [32, 576, 1024], P(('dp', 'tm'), 'mp'), parts along dimension 0, may hold values from -6 to 6
- queries: bfloat16 [2048, 1024], P(('dp', 'tm')), parts along dimension 0, may hold values from -6 to 6
- anchor_frame: int32 [2048], P(('dp', 'tm')), parts along dimension 0, may hold values from 0 to 15, as said below
- anchor_patch: int32 [2048], P(('dp', 'tm')), parts along dimension 0, may hold values from 0 to 575
- time_offset: float32 [2048, 8, 4], P(('dp', 'tm')), parts along dimension 0, may hold values from -1.99 to 1.99
- space_offset: float32 [2, 2048, 8, 4], P(None, ('dp', 'tm')), parts along dimension 1, may hold values from -3 to 3
- value_weight: bfloat16 [1024, 1024], replicated, may hold values from -0.1875 to 0.1875
- point_weight: bfloat16 [1024, 32], replicated, may hold values from -0.1875 to 0.1875
- point_bias: float32 [32], replicated, may hold values from -6 to 260
- output_weight: bfloat16 [1024, 1024], P('mp'), may hold values from -0.1875 to 0.1875
- project_weight: bfloat16 [1024, 3584], P(None, 'mp'), may hold values from -2 to 2
- norm_gain: float32 [3584], P('mp'), may hold values from 0.1 to 1.9
- query_weight: bfloat16 [3584, 3072], P(None, 'mp'), may hold values from -0.09375 to 0.09375
- query_bias: float32 [3072], P('mp'), may hold values from -6 to 40
- cache_weight: bfloat16 [3584, 1024], P(None, 'mp'), may hold values from -0.09375 to 0.09375
- cache_bias: float32 [1024], P('mp'), may hold values from -6 to 40
Outputs:
- attention: bfloat16 [2048, 3072], P(('dp', 'tm'), 'mp'), parts along dimension 0
- key_value: bfloat16 [2048, 1024], P(('dp', 'tm'), 'mp'), parts along dimension 0
There are 2 independent parts, one for each index of `dp`. A program takes and returns all parts, laid end to end along the dimension named above; an argument that names none is the same for every part. Nothing has to cross between parts.
Inputs may be any that keep to these rules, and one draw needn't show every extreme that they name: `anchor_frame`: the anchor frame of query q lies among the 4 frames that begin at (q // 256) * 4.
All inputs are finite; a program needn't handle non-finite values.
Results may differ from a plain program's by a relative error of at most 0.04.
Values may be sent and summed in bfloat16 or wider, within the bound.
A program may use at most 64 MiB of HBM per device.

v0:
```python
import jax
import jax.numpy as jnp
from jax import lax
from jax.sharding import PartitionSpec as P

AH = 8
POINTS = 4
GRID = 24
KVH = 4
HD = 128
GROUP = 7
rope_base = 1000000.0
epsilon = 1e-06
masked = -1e30


def with_halo(block, sides, width):
    for axis, dim in sides:
        count = lax.axis_size(axis)
        forward = [(i, i + 1) for i in range(count - 1)]
        backward = [(target, source) for source, target in forward]
        low = lax.ppermute(
            lax.slice_in_dim(block, block.shape[dim] - width, None, axis=dim), axis, forward
        )
        high = lax.ppermute(lax.slice_in_dim(block, 0, width, axis=dim), axis, backward)
        block = jnp.concatenate([low, block, high], axis=dim)
    return block


def rotate(vectors, positions):
    half_width = vectors.shape[-1] // 2
    frequency = rope_base ** (-2.0 * jnp.arange(half_width, dtype=jnp.float32) / vectors.shape[-1])
    angles = positions.astype(jnp.float32)[:, None] * frequency[None, :]
    cosine = jnp.cos(angles)[:, None, :]
    sine_part = jnp.sin(angles)[:, None, :]
    first_half = vectors[..., :half_width]
    second_half = vectors[..., half_width:]
    return jnp.concatenate(
        [
            first_half * cosine - second_half * sine_part,
            second_half * cosine + first_half * sine_part,
        ],
        axis=-1,
    )


def trilinear_corners(frame_pos, row_pos, column_pos, weight, frame_total, side):
    floor_frame = jnp.floor(frame_pos)
    floor_row = jnp.floor(row_pos)
    floor_column = jnp.floor(column_pos)
    frame_part = frame_pos - floor_frame
    row_part = row_pos - floor_row
    column_part = column_pos - floor_column
    frame_start = floor_frame.astype(jnp.int32)
    row_start = floor_row.astype(jnp.int32)
    column_start = floor_column.astype(jnp.int32)
    listing = []
    for frame_step in (0, 1):
        for row_step in (0, 1):
            for column_step in (0, 1):
                frame_cell = frame_start + frame_step
                row_cell = row_start + row_step
                column_cell = column_start + column_step
                portion = weight * (frame_part if frame_step else 1.0 - frame_part)
                portion = portion * (row_part if row_step else 1.0 - row_part)
                portion = portion * (column_part if column_step else 1.0 - column_part)
                inside = (
                    (frame_cell >= 0)
                    & (frame_cell < frame_total)
                    & (row_cell >= 0)
                    & (row_cell < side)
                )
                inside = inside & (column_cell >= 0) & (column_cell < side)
                portion = jnp.where(inside, portion, 0.0)
                patch_id = jnp.clip(row_cell, 0, side - 1) * side + jnp.clip(
                    column_cell, 0, side - 1
                )
                listing.append((frame_cell, patch_id, portion))
    return listing


def make_attend(query_turned, positions, head_map, scaling):

    def attend(state_in, members, first_row):
        key_rows, value_rows = members
        length = key_rows.shape[0]
        block_len = 512
        block_count = length // block_len
        key_blocks = key_rows.reshape(block_count, block_len, -1, HD)[:, :, head_map, :]
        value_blocks = value_rows.reshape(block_count, block_len, -1, HD)[:, :, head_map, :]
        block_starts = jnp.arange(block_count, dtype=jnp.int32) * block_len

        def advance(running, inputs):
            peak_score, denominator, numerator = running
            key_block, value_block, block_start = inputs
            scores = (
                jnp.einsum(
                    "qhd,nhd->hqn", query_turned, key_block, preferred_element_type=jnp.float32
                )
                * scaling
            )
            key_pos = block_start + jnp.arange(block_len, dtype=jnp.int32)
            allowed = key_pos[None, None, :] <= positions[None, :, None]
            scores = jnp.where(allowed, scores, masked)
            new_peak = jnp.maximum(peak_score, jnp.max(scores, axis=-1))
            weights = jnp.where(allowed, jnp.exp(scores - new_peak[..., None]), 0.0)
            rescale = jnp.exp(peak_score - new_peak)
            denominator = denominator * rescale + jnp.sum(weights, axis=-1)
            numerator = numerator * rescale[..., None] + jnp.einsum(
                "hqn,nhd->hqd",
                weights.astype(jnp.bfloat16),
                value_block,
                preferred_element_type=jnp.float32,
            )
            return ((new_peak, denominator, numerator), None)

        result, unused = lax.scan(advance, state_in, (key_blocks, value_blocks, block_starts))
        return result

    return attend


def local(
    features,
    queries,
    anchor_frame,
    anchor_patch,
    time_offset,
    space_offset,
    value_weight,
    point_weight,
    point_bias,
    output_weight,
    project_weight,
    norm_gain,
    query_weight,
    query_bias,
    cache_weight,
    cache_bias,
):
    groups = lax.axis_size("mp")
    group_index = lax.axis_index("mp")
    frame_index = lax.axis_index("tm")
    frames_here, patches_here, feature_width = features.shape
    rows_here = queries.shape[0]
    frame_total = frames_here * lax.axis_size("tm")
    patch_total = GRID * GRID
    head_width = feature_width // AH
    heads_here = AH // groups
    first_frame = frame_index * frames_here - 2
    projected = jnp.dot(
        features.reshape(frames_here * patches_here, feature_width),
        value_weight,
        preferred_element_type=jnp.float32,
    )
    projected = projected.astype(jnp.bfloat16).reshape(frames_here, patches_here, feature_width)
    logits = jnp.dot(queries, point_weight, preferred_element_type=jnp.float32) + point_bias
    point_share = jax.nn.softmax(logits.reshape(rows_here, AH, POINTS), axis=-1)
    frame_pos = anchor_frame.astype(jnp.float32)[:, None, None] + time_offset
    row_pos = (anchor_patch // GRID).astype(jnp.float32)[:, None, None] + space_offset[0]
    column_pos = (anchor_patch % GRID).astype(jnp.float32)[:, None, None] + space_offset[1]

    def own_slice(array):
        return lax.dynamic_slice_in_dim(array, group_index * heads_here, heads_here, 1)

    by_head = lax.all_to_all(projected, "mp", split_axis=2, concat_axis=1, tiled=True)
    padded = with_halo(by_head, (("tm", 0),), 2)
    lookup = padded.reshape(-1, heads_here, head_width)
    head_lane = jnp.arange(heads_here, dtype=jnp.int32)[None, :, None]
    running = jnp.zeros((rows_here, heads_here, head_width), jnp.float32)
    for frame_cell, patch_id, portion in trilinear_corners(
        own_slice(frame_pos),
        own_slice(row_pos),
        own_slice(column_pos),
        own_slice(point_share),
        frame_total,
        GRID,
    ):
        local_frame = jnp.clip(frame_cell - first_frame, 0, frames_here + 3)
        picked = lookup[local_frame * patch_total + patch_id, head_lane]
        running = running + jnp.sum(portion[..., None] * picked.astype(jnp.float32), axis=2)
    sampled = running.reshape(rows_here, heads_here * head_width).astype(jnp.bfloat16)
    head_terms = jnp.dot(sampled, output_weight, preferred_element_type=jnp.float32)
    head_mix = lax.psum(head_terms, "mp")
    abstract = (queries.astype(jnp.float32) + head_mix).astype(jnp.bfloat16)
    visual = jnp.dot(abstract, project_weight, preferred_element_type=jnp.float32)
    squares = lax.psum(jnp.sum(visual * visual, axis=1), "mp")
    model_width = query_weight.shape[0]
    normed = (visual * lax.rsqrt(squares / model_width + epsilon)[:, None] * norm_gain).astype(
        jnp.bfloat16
    )
    shard_piece = lax.all_gather(normed, "mp", axis=1, tiled=True)
    query_sum = jnp.dot(shard_piece, query_weight, preferred_element_type=jnp.float32)
    cache_sum = jnp.dot(shard_piece, cache_weight, preferred_element_type=jnp.float32)
    positions = frame_index * rows_here + jnp.arange(rows_here, dtype=jnp.int32)
    query_heads = query_weight.shape[1] // HD
    query_turned = rotate(
        (query_sum + query_bias).reshape(rows_here, query_heads, HD), positions
    ).astype(jnp.bfloat16)
    cache_heads = cache_weight.shape[1] // HD
    cache_state = (cache_sum + cache_bias).reshape(rows_here, cache_heads, HD)
    is_key = group_index * cache_heads + jnp.arange(cache_heads, dtype=jnp.int32) < KVH
    cache_state = jnp.where(is_key[None, :, None], rotate(cache_state, positions), cache_state)
    key_value = cache_state.reshape(rows_here, cache_heads * HD).astype(jnp.bfloat16)
    cache_all = lax.all_gather(key_value, "mp", axis=1, tiled=True)
    key_rows = cache_all[:, : KVH * HD]
    value_rows = cache_all[:, KVH * HD :]
    own_heads = (group_index * query_heads + jnp.arange(query_heads, dtype=jnp.int32)) // GROUP
    scaling = HD ** (-0.5)
    initial = (
        jnp.full((query_heads, rows_here), masked, jnp.float32),
        jnp.zeros((query_heads, rows_here), jnp.float32),
        jnp.zeros((query_heads, rows_here, HD), jnp.float32),
    )
    span_heads = min(KVH, (query_heads - 1) // GROUP + 2)
    lowest = jnp.minimum(group_index * query_heads // GROUP, KVH - span_heads)
    key_rows = lax.dynamic_slice_in_dim(key_rows, lowest * HD, span_heads * HD, 1)
    value_rows = lax.dynamic_slice_in_dim(value_rows, lowest * HD, span_heads * HD, 1)
    attend = make_attend(query_turned, positions, own_heads - lowest, scaling)
    peak_score, denominator, numerator = attend(
        initial,
        (
            lax.all_gather(key_rows, "tm", axis=0, tiled=True),
            lax.all_gather(value_rows, "tm", axis=0, tiled=True),
        ),
        jnp.int32(0),
    )
    attention = (
        (numerator / denominator[..., None])
        .transpose(1, 0, 2)
        .reshape(rows_here, query_heads * HD)
        .astype(jnp.bfloat16)
    )
    return (attention, key_value)


def solution(mesh):
    return jax.shard_map(
        local,
        mesh=mesh,
        in_specs=(
            P(("dp", "tm"), "mp", None),
            P(("dp", "tm"), None),
            P(("dp", "tm")),
            P(("dp", "tm")),
            P(("dp", "tm"), None, None),
            P(None, ("dp", "tm"), None, None),
            P(),
            P(),
            P(),
            P("mp", None),
            P(None, "mp"),
            P("mp"),
            P(None, "mp"),
            P("mp"),
            P(None, "mp"),
            P("mp"),
        ),
        out_specs=(P(("dp", "tm"), "mp"), P(("dp", "tm"), "mp")),
        check_vma=False,
    )
```

profile of v0, /device:TPU:0, one launch (start us, length us, event | category | flops | bytes accessed | tf_op | source)
XLA Modules:
  0.0 499.3 jit_solution(2481878164457223012)
XLA Ops:
  8.8 2.7 convolution_convert_fusion
  14.0 4.6 all-to-all-start
  20.1 24.9 %all-to-all-done = bf16[4,144,1024]{1,0,2:T(4,128)(2,1)} async-done(((bf16[4,144,1024]{1,0,2:T(4,128)(2,1)}), bf16[4,144,1024]{1,0,2:T(4,128)(2,1)}, u32[]{:S(2)}, u32[]{:S(2)}) %all-to-all-start) | async-done | bytes 1179680 | tf_op jit(solution)/shard_map/all_to_all | solution.py:166
  45.0 4.7 fusion.73
  49.8 3.5 copy.68
  53.3 5.1 %collective-permute-start = (bf16[2,576,256]{2,1,0:T(8,128)(2,1)}, bf16[2,576,256]{2,1,0:T(8,128)(2,1)}, u32[]{:S(2)}, u32[]{:S(2)}) collective-permute-start(bf16[2,576,256]{2,1,0:T(8,128)(2,1)} %bitcast.167), channel_id=1, source_target_pairs={{0,4},{4,8},{8,12},{1,5},{5,9},{9,13},{2,6},{6,10},{10,14},{3,7},{... | collective-permute-start | bytes 1769480 | tf_op jit(solution)/shard_map/ppermute | solution.py:22
  72.0 3.1 copy.69
  76.9 2.9 pad_maximum_fusion
  79.9 5.7 %reshape.215 = bf16[4608,2,128]{2,1,0:T(2,128)(2,1)} reshape(bf16[8,576,256]{2,1,0:T(8,128)(2,1)} %pad_maximum_fusion) | data formatting | bytes 4718592 | tf_op jit(solution)/shard_map/reshape | solution.py:168
  85.6 32.5 %gather_fusion = bf16[2048,128]{1,0:T(8,128)(2,1)} fusion(bf16[4608,2,128]{2,1,0:T(2,128)(2,1)} %reshape.215, s32[2048]{0:T(1024)S(1)} %reshape.224), kind=kCustom, calls=%fused_computation | custom fusion | bytes 1064960 | tf_op jit(solution)/shard_map/gather | solution.py:180
  118.1 32.4 %gather_fusion.1 = bf16[2048,128]{1,0:T(8,128)(2,1)} fusion(bf16[4608,2,128]{2,1,0:T(2,128)(2,1)} %reshape.215, s32[2048]{0:T(1024)S(1)} %reshape.230), kind=kCustom, calls=%fused_computation.1 | custom fusion | bytes 1064960 | tf_op jit(solution)/shard_map/gather | solution.py:180
  150.5 32.5 %gather_fusion.2 = bf16[2048,128]{1,0:T(8,128)(2,1)} fusion(bf16[4608,2,128]{2,1,0:T(2,128)(2,1)} %reshape.215, s32[2048]{0:T(1024)S(1)} %reshape.236), kind=kCustom, calls=%fused_computation.2 | custom fusion | bytes 1064960 | tf_op jit(solution)/shard_map/gather | solution.py:180
  183.0 32.3 %gather_fusion.3 = bf16[2048,128]{1,0:T(8,128)(2,1)} fusion(bf16[4608,2,128]{2,1,0:T(2,128)(2,1)} %reshape.215, s32[2048]{0:T(1024)S(1)} %reshape.242), kind=kCustom, calls=%fused_computation.3 | custom fusion | bytes 1064960 | tf_op jit(solution)/shard_map/gather | solution.py:180
  215.3 32.4 %gather_fusion.4 = bf16[2048,128]{1,0:T(8,128)(2,1)} fusion(bf16[4608,2,128]{2,1,0:T(2,128)(2,1)} %reshape.215, s32[2048]{0:T(1024)S(1)} %reshape.248), kind=kCustom, calls=%fused_computation.4 | custom fusion | bytes 1064960 | tf_op jit(solution)/shard_map/gather | solution.py:180
  247.7 32.3 %gather_fusion.5 = bf16[2048,128]{1,0:T(8,128)(2,1)} fusion(bf16[4608,2,128]{2,1,0:T(2,128)(2,1)} %reshape.215, s32[2048]{0:T(1024)S(1)} %reshape.254), kind=kCustom, calls=%fused_computation.5 | custom fusion | bytes 1064960 | tf_op jit(solution)/shard_map/gather | solution.py:180
  280.0 23.0 %gather_fusion.6 = bf16[2048,128]{1,0:T(8,128)(2,1)S(1)} fusion(bf16[4608,2,128]{2,1,0:T(2,128)(2,1)} %reshape.215, s32[2048]{0:T(1024)S(1)} %reshape.260), kind=kCustom, calls=%fused_computation.6 | custom fusion | bytes 1064960 | tf_op jit(solution)/shard_map/gather | solution.py:180
  303.0 22.9 %gather_fusion.7 = bf16[2048,128]{1,0:T(8,128)(2,1)S(1)} fusion(bf16[4608,2,128]{2,1,0:T(2,128)(2,1)} %reshape.215, s32[2048]{0:T(1024)S(1)} %reshape.266), kind=kCustom, calls=%fused_computation.7 | custom fusion | bytes 1064960 | tf_op jit(solution)/shard_map/gather | solution.py:180
  326.0 3.7 fusion.28
  329.7 3.3 fusion.26
  339.1 36.6 %all-reduce.2.cloned.1.call-done = f32[256,1024]{1,0:T(8,128)} async-done(((f32[256,1024]{1,0:T(8,128)}), f32[256,1024]{1,0:T(8,128)}) %all-reduce.2.cloned.1.call-update) | async-done | bytes 1048592 | tf_op jit(solution)/shard_map/psum | solution.py:184
  378.3 5.9 %psum.15 = f32[256]{0:T(256)S(1)} all-reduce(f32[256]{0:T(256)S(1)} %get-tuple-element.180), channel_id=1, replica_groups=mesh['dp'=2,'tm'=4,'mp'=4] {'mp'}, use_global_device_ids=true, to_apply=%region_12.13 | all-reduce | flops 256 | bytes 2048 | tf_op jit(solution)/shard_map/psum | solution.py:187
  386.9 19.8 %all-gather.2.cloned.1.call-done = bf16[256,3584]{1,0:T(8,128)(2,1)} async-done(((bf16[256,896]{1,0:T(8,128)(2,1)}), bf16[256,3584]{1,0:T(8,128)(2,1)}) %all-gather.2.cloned.1.call-update) | async-done | bytes 1835024 | tf_op jit(solution)/shard_map/all_gather | solution.py:192
  406.7 2.9 convolution_add_fusion.1
  409.8 7.2 %all_gather.13 = bf16[256,1024]{0,1:T(8,128)(2,1)S(1)} all-gather(bf16[256,256]{0,1:T(8,128)(2,1)S(1)} %fusion.31), channel_id=1, replica_groups=mesh['dp'=2,'tm'=4,'mp'=4] {'mp'}, dimensions={1}, use_global_device_ids=true | all-gather | bytes 655360 | tf_op jit(solution)/shard_map/all_gather | solution.py:205
  417.7 5.6 %convolution_add_fusion = f32[256,768]{1,0:T(8,128)} fusion(bf16[256,3584]{1,0:T(8,128)(2,1)} %all-gather.2.cloned.1.call-done, bf16[3584,768]{1,0:T(8,128)(2,1)} %param.30, f32[768]{0:T(1024)S(1)} %copy-done.23), kind=kOutput, calls=%fused_computation.39 | convolution fusion | flops 1409482752 | bytes 8129536 | tf_op jit(solution)/shard_map/dot_general | solution.py:193
  425.9 16.1 %all_gather.15 = bf16[1024,256]{0,1:T(8,128)(2,1)S(1)} all-gather(bf16[256,256]{0,1:T(8,128)(2,1)S(1)} %constant_dynamic-slice_fusion), channel_id=1, replica_groups=mesh['dp'=2,'tm'=4,'mp'=4] {'tm'}, dimensions={0}, use_global_device_ids=true | all-gather | bytes 655360 | tf_op jit(solution)/shard_map/all_gather | solution.py:224
  443.7 16.0 %all_gather.14 = bf16[1024,256]{0,1:T(8,128)(2,1)S(1)} all-gather(bf16[256,256]{0,1:T(8,128)(2,1)S(1)} %constant_dynamic-slice_fusion.1), channel_id=1, replica_groups=mesh['dp'=2,'tm'=4,'mp'=4] {'tm'}, dimensions={0}, use_global_device_ids=true | all-gather | bytes 655360 | tf_op jit(solution)/shard_map/all_gather | solution.py:223
  466.4 23.6 %while.15 = (s32[]{:T(128)}, f32[6,256]{1,0:T(8,128)S(1)}, f32[6,256]{1,0:T(8,128)S(1)}, f32[6,256,128]{2,1,0:T(8,128)}, s32[2]{0:T(128)}, /*index=5*/bf16[2,512...) while((s32[]{:T(128)}, f32[6,256]{1,0:T(8,128)S(1)}, ...), condition=%wide.region_16.17_spmd.clone, body=%wide.region_13.16_spmd.clone.sunk | while | flops 413606144 | bytes 32480480 | solution.py:117
  468.4 3.5 fusion.96
  471.9 2.8 fusion.97
  480.2 3.5 fusion.96
  483.7 2.8 fusion.97
  (154 shorter events, 57.2 us)
Async XLA Ops:
  7.2 1.6 copy-start
  13.9 4.7 copy-start.2
  14.0 4.7 copy-start.17
  14.0 4.7 copy-start.22
  14.0 5.1 %copy-start.21 = (s32[256]{0:T(256)S(1)}, s32[256]{0:T(256)}, u32[]{:S(2)}) copy-start(s32[256]{0:T(256)} %param.20) | copy-start | bytes 3076
  14.0 5.1 %copy-start.20 = (s32[256]{0:T(256)S(1)}, s32[256]{0:T(256)}, u32[]{:S(2)}) copy-start(s32[256]{0:T(256)} %param.21) | copy-start | bytes 3076
  14.0 5.1 %copy-start.16 = (f32[2,256,8,4]{1,3,2,0:T(4,128)S(1)}, f32[2,256,8,4]{1,3,2,0:T(4,128)}, u32[]{:S(2)}) copy-start(f32[2,256,8,4]{1,3,2,0:T(4,128)} %param.23) | copy-start | bytes 196612
  14.0 5.1 %copy-start.18 = (f32[256,8,4]{0,2,1:T(4,128)S(1)}, f32[256,8,4]{0,2,1:T(4,128)}, u32[]{:S(2)}) copy-start(f32[256,8,4]{0,2,1:T(4,128)} %param.22) | copy-start | bytes 98308
  14.0 31.0 %all-to-all-start = ((bf16[4,144,1024]{1,0,2:T(4,128)(2,1)}), bf16[4,144,1024]{1,0,2:T(4,128)(2,1)}, u32[]{:S(2)}, u32[]{:S(2)}) async-start(bf16[4,144,1024]{1,0,2:T(4,128)(2,1)} %copy.67), calls=%async_computation | async-start | bytes 4194304 | tf_op jit(solution)/shard_map/all_to_all | solution.py:166
  18.6 357.1 %all-reduce.2.cloned.1.call-start = ((), (), s32[]{:S(2)}) async-start(), calls=%async_computation.1 | async-start | bytes 2097152 | tf_op jit(solution)/shard_map/psum | solution.py:184
  53.3 21.8 %collective-permute-start = (bf16[2,576,256]{2,1,0:T(8,128)(2,1)}, bf16[2,576,256]{2,1,0:T(8,128)(2,1)}, u32[]{:S(2)}, u32[]{:S(2)}) collective-permute-start(bf16[2,576,256]{2,1,0:T(8,128)(2,1)} %bitcast.167), channel_id=1, source_target_pairs={{0,4},{4,8},{8,12},{1,5},{5,9},{9,13},{2,6},{6,10},{10,14},{3,7},{... | collective-permute-start | bytes 1769480 | tf_op jit(solution)/shard_map/ppermute | solution.py:22
  60.3 16.7 %collective-permute-start.1 = (bf16[2,576,256]{2,1,0:T(8,128)(2,1)}, bf16[2,576,256]{2,1,0:T(8,128)(2,1)}, u32[]{:S(2)}, u32[]{:S(2)}) collective-permute-start(bf16[2,576,256]{2,1,0:T(8,128)(2,1)} %bitcast.168), channel_id=1, source_target_pairs={{4,0},{8,4},{12,8},{5,1},{9,5},{13,9},{6,2},{10,6},{14,10},{7,3},{... | collective-permute-start | bytes 1769480 | tf_op jit(solution)/shard_map/ppermute | solution.py:25
  303.0 22.9 %copy-start.8 = (f32[256,2,4]{2,1,0:T(2,128)S(1)}, f32[256,2,4]{2,1,0:T(2,128)}, u32[]{:S(2)}) copy-start(f32[256,2,4]{2,1,0:T(2,128)} %copy.66) | copy-start | bytes 24580
  325.9 3.8 copy-start.6
  325.9 3.8 copy-start.7
  325.9 7.0 %copy-start.4 = (bf16[2048,128]{1,0:T(8,128)(2,1)S(1)}, bf16[2048,128]{1,0:T(8,128)(2,1)}, u32[]{:S(2)}) copy-start(bf16[2048,128]{1,0:T(8,128)(2,1)} %gather_fusion.4) | copy-start | bytes 1572868
  325.9 7.0 %copy-start.5 = (bf16[2048,128]{1,0:T(8,128)(2,1)S(1)}, bf16[2048,128]{1,0:T(8,128)(2,1)}, u32[]{:S(2)}) copy-start(bf16[2048,128]{1,0:T(8,128)(2,1)} %gather_fusion.5) | copy-start | bytes 1572868
  325.9 7.0 %copy-start.9 = (f32[256,2,4]{2,1,0:T(2,128)S(1)}, f32[256,2,4]{2,1,0:T(2,128)}, u32[]{:S(2)}) copy-start(f32[256,2,4]{2,1,0:T(2,128)} %copy.80) | copy-start | bytes 24580
  325.9 7.0 %copy-start.10 = (f32[256,2,4]{2,1,0:T(2,128)S(1)}, f32[256,2,4]{2,1,0:T(2,128)}, u32[]{:S(2)}) copy-start(f32[256,2,4]{2,1,0:T(2,128)} %copy.78) | copy-start | bytes 24580
  329.6 5.4 %copy-start.11 = (f32[256,2,4]{2,1,0:T(2,128)S(1)}, f32[256,2,4]{2,1,0:T(2,128)}, u32[]{:S(2)}) copy-start(f32[256,2,4]{2,1,0:T(2,128)} %copy.82) | copy-start | bytes 24580
  329.6 5.4 %copy-start.12 = (f32[256,2,4]{2,1,0:T(2,128)S(1)}, f32[256,2,4]{2,1,0:T(2,128)}, u32[]{:S(2)}) copy-start(f32[256,2,4]{2,1,0:T(2,128)} %copy.84) | copy-start | bytes 24580
  335.0 2.5 copy-start.15
  337.0 38.7 %copy-start.3 = (bf16[256,1024]{1,0:T(8,128)(2,1)S(1)}, bf16[256,1024]{1,0:T(8,128)(2,1)}, u32[]{:S(2)}) copy-start(bf16[256,1024]{1,0:T(8,128)(2,1)} %param.19) | copy-start | bytes 1572868
  338.8 45.5 %copy-start.19 = (f32[896]{0:T(1024)S(1)}, f32[896]{0:T(1024)}, u32[]{:S(2)}) copy-start(f32[896]{0:T(1024)} %param.29) | copy-start | bytes 10756
  338.8 67.9 %all-gather.2.cloned.1.call-start = ((), (), s32[]{:S(2)}) async-start(), calls=%async_computation.2 | async-start | bytes 2293760 | tf_op jit(solution)/shard_map/all_gather | solution.py:192
  386.9 30.8 %copy-start.23 = (f32[768]{0:T(1024)S(1)}, f32[768]{0:T(1024)}, u32[]{:S(2)}) copy-start(f32[768]{0:T(1024)} %param.31) | copy-start | bytes 9220
  468.4 6.3 %copy-start.13 = (f32[6,256,128]{2,1,0:T(8,128)S(1)}, f32[6,256,128]{2,1,0:T(8,128)}, u32[]{:S(2)}) copy-start(f32[6,256,128]{2,1,0:T(8,128)} %get-tuple-element.267) | copy-start | bytes 2359300 | tf_op jit(solution)/shard_map/while
  471.9 2.8 copy-start.1
  477.3 0.9 copy-start.14
  480.2 6.3 %copy-start.13 = (f32[6,256,128]{2,1,0:T(8,128)S(1)}, f32[6,256,128]{2,1,0:T(8,128)}, u32[]{:S(2)}) copy-start(f32[6,256,128]{2,1,0:T(8,128)} %get-tuple-element.267) | copy-start | bytes 2359300 | tf_op jit(solution)/shard_map/while
  483.7 2.8 copy-start.1
  489.1 0.9 copy-start.14
Sparse Core Ops, SparseCore 0:
  338.9 36.7 all-reduce.1
  385.4 21.2 all-gather.1
where the time goes:
time: 502 us; the launch traced here: 499 us
  local copies, waits for them, and re-layouts  293 us (58%)
  waiting for transfers between devices  83.2 us (17%)
  blocking collectives  45.1 us (9%)
  matrix products  27.4 us (5%)
  other arithmetic  24.5 us (5%)
  between operations  14.8 us (3%)
  starting transfers between devices  11.3 us (2%)
    gather x8, local copies, waits for them, and re-layouts, local(): picked = lookup[local_frame * patch_total + patch_id, head_lane]  240 us
    psum x1, waiting for transfers between devices, local(): head_mix = lax.psum(head_terms, 'mp')  36.6 us
    all_to_all x1, waiting for transfers between devices, local(): lax.all_to_all(projected, 'mp', split_axis=2, concat_axis=1, tiled=True)  24.9 us
    all_gather x1, waiting for transfers between devices, local(): shard_piece = lax.all_gather(normed, 'mp', axis=1, tiled=True)  19.8 us
    all_gather x1, blocking collectives, local(): lax.all_gather(value_rows, 'tm', axis=0, tiled=True)  16.1 us
    all_gather x1, blocking collectives, local(): lax.all_gather(key_rows, 'tm', axis=0, tiled=True)  16 us
    reduce_sum x4, other arithmetic, local(): jnp.sum(portion[..., None] * picked.astype(jnp.float32), axis=2)  10.9 us
  transfers between devices with their start and end apart: 5, of which 4 were waited for; matrix products, arithmetic and copies ran while one was open for 4% of the time, Pallas kernels for 0%

commit v1 on v0

--- a/solution.py
+++ b/solution.py
@@ -163,7 +163,18 @@
     def own_slice(array):
         return lax.dynamic_slice_in_dim(array, group_index * heads_here, heads_here, 1)
 
-    by_head = lax.all_to_all(projected, "mp", split_axis=2, concat_axis=1, tiled=True)
+    ways, here = (lax.axis_size("mp"), lax.axis_index("mp"))
+    width_2 = projected.shape[2] // ways
+    shape = list(projected.shape)
+    shape[2] = width_2
+    height = shape[1]
+    shape[1] = height * ways
+    by_head = jnp.zeros(shape, projected.dtype)
+    for mask in range(ways):
+        part = lax.dynamic_slice_in_dim(projected, (here ^ mask) * width_2, width_2, axis=2)
+        if mask:
+            part = lax.ppermute(part, "mp", [(d, d ^ mask) for d in range(ways)])
+        by_head = lax.dynamic_update_slice_in_dim(by_head, part, (here ^ mask) * height, axis=1)
     padded = with_halo(by_head, (("tm", 0),), 2)
     lookup = padded.reshape(-1, heads_here, head_width)
     head_lane = jnp.arange(heads_here, dtype=jnp.int32)[None, :, None]

time: 502 us -> 483 us (0.962)
  waiting for transfers between devices: 83.2 us -> 64.1 us
    all_to_all x1 -> x0, waiting for transfers between devices: 24.9 us -> none  [local(): lax.all_to_all(projected, 'mp', split_axis=2, concat_axis=1, tiled=True)]
    concatenate x16, local copies, waits for them, and re-layouts: 4.14 us -> 17.1 us  [local(): picked = lookup[local_frame * patch_total + patch_id, head_lane]]
    slice x2 -> x1, local copies, waits for them, and re-layouts: 8.29 us -> 1.1 us  [with_halo(): lax.slice_in_dim(block, block.shape[dim] - width, None, axis=dim)]
    ppermute x0 -> x3, waiting for transfers between devices: none -> 5.56 us  [local(): part = lax.ppermute(part, 'mp', [(d, d ^ mask) for d in range(ways)])]
  transfers between devices with their start and end apart: 5 -> 7, of which waited for: 4 -> 4; matrix products, arithmetic and copies ran while one was open for 4% -> 6% of each run, Pallas kernels for 0% -> 0%
where the time goes in v1:
time: 483 us; the launch traced here: 480 us
  local copies, waits for them, and re-layouts  294 us (61%)
  waiting for transfers between devices  64.1 us (13%)
  blocking collectives  45.1 us (9%)
  matrix products  28.5 us (6%)
  other arithmetic  24.5 us (5%)
  between operations  14.8 us (3%)
  starting transfers between devices  8.92 us (2%)
    gather x8, local copies, waits for them, and re-layouts, local(): picked = lookup[local_frame * patch_total + patch_id, head_lane]  240 us
    psum x1, waiting for transfers between devices, local(): head_mix = lax.psum(head_terms, 'mp')  38.6 us
    all_gather x1, waiting for transfers between devices, local(): shard_piece = lax.all_gather(normed, 'mp', axis=1, tiled=True)  19.9 us
    concatenate x16, local copies, waits for them, and re-layouts, local(): picked = lookup[local_frame * patch_total + patch_id, head_lane]  17.1 us
    all_gather x1, blocking collectives, local(): lax.all_gather(value_rows, 'tm', axis=0, tiled=True)  16.1 us
    all_gather x1, blocking collectives, local(): lax.all_gather(key_rows, 'tm', axis=0, tiled=True)  16 us
  transfers between devices with their start and end apart: 7, of which 4 were waited for; matrix products, arithmetic and copies ran while one was open for 6% of the time, Pallas kernels for 0%

profile of v1, /device:TPU:0, one launch (start us, length us, event | category | flops | bytes accessed | tf_op | source)
XLA Modules:
  0.0 480.2 jit_solution(1775927877947702237)
XLA Ops:
  8.8 2.7 convolution_convert_fusion
  13.0 2.5 collective-permute-start.1
  24.7 5.0 %collective-permute-done.2 = bf16[4,144,256]{2,1,0:T(8,128)(2,1)} collective-permute-done((bf16[4,144,256]{2,1,0:T(8,128)(2,1)}, bf16[4,144,256]{2,1,0:T(8,128)(2,1)}, u32[]{:S(2)}, u32[]{:S(2)}) %collective-permute-start.2) | collective-permute-done | bytes 294944 | tf_op jit(solution)/shard_map/ppermute | solution.py:176
  31.8 4.2 collective-permute-start.3
  57.8 2.9 pad_maximum_fusion
  60.8 5.7 %reshape.213 = bf16[4608,2,128]{2,1,0:T(2,128)(2,1)} reshape(bf16[8,576,256]{2,1,0:T(8,128)(2,1)} %pad_maximum_fusion) | data formatting | bytes 4718592 | tf_op jit(solution)/shard_map/reshape | solution.py:179
  66.5 32.1 %gather_fusion = bf16[2048,128]{1,0:T(8,128)(2,1)} fusion(bf16[4608,2,128]{2,1,0:T(2,128)(2,1)} %reshape.213, s32[2048]{0:T(1024)S(1)} %reshape.222), kind=kCustom, calls=%fused_computation | custom fusion | bytes 1064960 | tf_op jit(solution)/shard_map/gather | solution.py:191
  98.6 32.3 %gather_fusion.1 = bf16[2048,128]{1,0:T(8,128)(2,1)} fusion(bf16[4608,2,128]{2,1,0:T(2,128)(2,1)} %reshape.213, s32[2048]{0:T(1024)S(1)} %reshape.228), kind=kCustom, calls=%fused_computation.1 | custom fusion | bytes 1064960 | tf_op jit(solution)/shard_map/gather | solution.py:191
  130.9 32.3 %gather_fusion.2 = bf16[2048,128]{1,0:T(8,128)(2,1)} fusion(bf16[4608,2,128]{2,1,0:T(2,128)(2,1)} %reshape.213, s32[2048]{0:T(1024)S(1)} %reshape.234), kind=kCustom, calls=%fused_computation.2 | custom fusion | bytes 1064960 | tf_op jit(solution)/shard_map/gather | solution.py:191
  163.3 32.4 %gather_fusion.3 = bf16[2048,128]{1,0:T(8,128)(2,1)} fusion(bf16[4608,2,128]{2,1,0:T(2,128)(2,1)} %reshape.213, s32[2048]{0:T(1024)S(1)} %reshape.240), kind=kCustom, calls=%fused_computation.3 | custom fusion | bytes 1064960 | tf_op jit(solution)/shard_map/gather | solution.py:191
  195.6 32.3 %gather_fusion.4 = bf16[2048,128]{1,0:T(8,128)(2,1)} fusion(bf16[4608,2,128]{2,1,0:T(2,128)(2,1)} %reshape.213, s32[2048]{0:T(1024)S(1)} %reshape.246), kind=kCustom, calls=%fused_computation.4 | custom fusion | bytes 1064960 | tf_op jit(solution)/shard_map/gather | solution.py:191
  227.9 32.3 %gather_fusion.5 = bf16[2048,128]{1,0:T(8,128)(2,1)} fusion(bf16[4608,2,128]{2,1,0:T(2,128)(2,1)} %reshape.213, s32[2048]{0:T(1024)S(1)} %reshape.252), kind=kCustom, calls=%fused_computation.5 | custom fusion | bytes 1064960 | tf_op jit(solution)/shard_map/gather | solution.py:191
  260.2 23.0 %gather_fusion.6 = bf16[2048,128]{1,0:T(8,128)(2,1)S(1)} fusion(bf16[4608,2,128]{2,1,0:T(2,128)(2,1)} %reshape.213, s32[2048]{0:T(1024)S(1)} %reshape.258), kind=kCustom, calls=%fused_computation.6 | custom fusion | bytes 1064960 | tf_op jit(solution)/shard_map/gather | solution.py:191
  283.2 23.0 %gather_fusion.7 = bf16[2048,128]{1,0:T(8,128)(2,1)S(1)} fusion(bf16[4608,2,128]{2,1,0:T(2,128)(2,1)} %reshape.213, s32[2048]{0:T(1024)S(1)} %reshape.264), kind=kCustom, calls=%fused_computation.7 | custom fusion | bytes 1064960 | tf_op jit(solution)/shard_map/gather | solution.py:191
  306.3 3.7 fusion.28
  318.1 38.6 %all-reduce.2.cloned.1.call-done = f32[256,1024]{1,0:T(8,128)} async-done(((f32[256,1024]{1,0:T(8,128)}), f32[256,1024]{1,0:T(8,128)}) %all-reduce.2.cloned.1.call-update) | async-done | bytes 1048592 | tf_op jit(solution)/shard_map/psum | solution.py:195
  356.7 2.6 multiply_reduce_fusion
  359.3 5.9 %psum.15 = f32[256]{0:T(256)S(1)} all-reduce(f32[256]{0:T(256)S(1)} %get-tuple-element.173), channel_id=1, replica_groups=mesh['dp'=2,'tm'=4,'mp'=4] {'mp'}, use_global_device_ids=true, to_apply=%region_12.13 | all-reduce | flops 256 | bytes 2048 | tf_op jit(solution)/shard_map/psum | solution.py:198
  367.8 19.9 %all-gather.2.cloned.1.call-done = bf16[256,3584]{1,0:T(8,128)(2,1)} async-done(((bf16[256,896]{1,0:T(8,128)(2,1)}), bf16[256,3584]{1,0:T(8,128)(2,1)}) %all-gather.2.cloned.1.call-update) | async-done | bytes 1835024 | tf_op jit(solution)/shard_map/all_gather | solution.py:203
  387.7 2.9 convolution_add_fusion.1
  390.8 7.2 %all_gather.13 = bf16[256,1024]{0,1:T(8,128)(2,1)S(1)} all-gather(bf16[256,256]{0,1:T(8,128)(2,1)S(1)} %fusion.31), channel_id=1, replica_groups=mesh['dp'=2,'tm'=4,'mp'=4] {'mp'}, dimensions={1}, use_global_device_ids=true | all-gather | bytes 655360 | tf_op jit(solution)/shard_map/all_gather | solution.py:216
  398.7 5.6 %convolution_add_fusion = f32[256,768]{1,0:T(8,128)} fusion(bf16[256,3584]{1,0:T(8,128)(2,1)} %all-gather.2.cloned.1.call-done, bf16[3584,768]{1,0:T(8,128)(2,1)} %param.30, f32[768]{0:T(1024)S(1)} %copy-done.24), kind=kOutput, calls=%fused_computation.39 | convolution fusion | flops 1409482752 | bytes 8129536 | tf_op jit(solution)/shard_map/dot_general | solution.py:204
  406.9 16.1 %all_gather.15 = bf16[1024,256]{0,1:T(8,128)(2,1)S(1)} all-gather(bf16[256,256]{0,1:T(8,128)(2,1)S(1)} %constant_dynamic-slice_fusion), channel_id=1, replica_groups=mesh['dp'=2,'tm'=4,'mp'=4] {'tm'}, dimensions={0}, use_global_device_ids=true | all-gather | bytes 655360 | tf_op jit(solution)/shard_map/all_gather | solution.py:235
  424.7 16.0 %all_gather.14 = bf16[1024,256]{0,1:T(8,128)(2,1)S(1)} all-gather(bf16[256,256]{0,1:T(8,128)(2,1)S(1)} %constant_dynamic-slice_fusion.1), channel_id=1, replica_groups=mesh['dp'=2,'tm'=4,'mp'=4] {'tm'}, dimensions={0}, use_global_device_ids=true | all-gather | bytes 655360 | tf_op jit(solution)/shard_map/all_gather | solution.py:234
  443.3 2.1 gather_fusion.9
  447.4 23.5 %while.15 = (s32[]{:T(128)}, f32[6,256]{1,0:T(8,128)S(1)}, f32[6,256]{1,0:T(8,128)S(1)}, f32[6,256,128]{2,1,0:T(8,128)}, s32[2]{0:T(128)}, /*index=5*/bf16[2,512...) while((s32[]{:T(128)}, f32[6,256]{1,0:T(8,128)S(1)}, ...), condition=%wide.region_16.17_spmd.clone, body=%wide.region_13.16_spmd.clone.sunk | while | flops 413606144 | bytes 32480480 | solution.py:117
  449.4 3.5 fusion.96
  452.9 2.8 fusion.97
  455.7 2.6 fusion.99
  461.2 3.5 fusion.96
  464.7 2.8 fusion.97
  467.5 2.6 fusion.99
  (161 shorter events, 64.4 us)
Async XLA Ops:
  7.2 349.5 %all-reduce.2.cloned.1.call-start = ((), (), s32[]{:S(2)}) async-start(), calls=%async_computation | async-start | bytes 2097152 | tf_op jit(solution)/shard_map/psum | solution.py:195
  11.4 4.2 copy-start.18
  11.4 4.2 copy-start.23
  11.4 5.6 %copy-start.17 = (f32[2,256,8,4]{1,3,2,0:T(4,128)S(1)}, f32[2,256,8,4]{1,3,2,0:T(4,128)}, u32[]{:S(2)}) copy-start(f32[2,256,8,4]{1,3,2,0:T(4,128)} %param.23) | copy-start | bytes 196612
  11.5 5.6 %copy-start.21 = (s32[256]{0:T(256)S(1)}, s32[256]{0:T(256)}, u32[]{:S(2)}) copy-start(s32[256]{0:T(256)} %param.21) | copy-start | bytes 3076
  11.5 5.7 %copy-start.22 = (s32[256]{0:T(256)S(1)}, s32[256]{0:T(256)}, u32[]{:S(2)}) copy-start(s32[256]{0:T(256)} %param.20) | copy-start | bytes 3076
  11.5 5.7 %copy-start.19 = (f32[256,8,4]{0,2,1:T(4,128)S(1)}, f32[256,8,4]{0,2,1:T(4,128)}, u32[]{:S(2)}) copy-start(f32[256,8,4]{0,2,1:T(4,128)} %param.22) | copy-start | bytes 98308
  12.6 9.6 %collective-permute-start = (bf16[4,144,256]{2,1,0:T(8,128)(2,1)}, bf16[4,144,256]{2,1,0:T(8,128)(2,1)}, u32[]{:S(2)}, u32[]{:S(2)}) collective-permute-start(bf16[4,144,256]{2,1,0:T(8,128)(2,1)} %get-tuple-element.144), channel_id=1, source_target_pairs={{0,1},{1,0},{2,3},{3,2},{4,5},{5,4},{6,7},{7,6},{8,9},{9,8},{10,11... | collective-permute-start | bytes 884744 | tf_op jit(solution)/shard_map/ppermute | solution.py:176
  13.0 10.7 %collective-permute-start.1 = (bf16[4,144,256]{2,1,0:T(8,128)(2,1)}, bf16[4,144,256]{2,1,0:T(8,128)(2,1)}, u32[]{:S(2)}, u32[]{:S(2)}) collective-permute-start(bf16[4,144,256]{2,1,0:T(8,128)(2,1)} %get-tuple-element.143), channel_id=1, source_target_pairs={{0,2},{1,3},{2,0},{3,1},{4,6},{5,7},{6,4},{7,5},{8,10},{9,11},{10,... | collective-permute-start | bytes 884744 | tf_op jit(solution)/shard_map/ppermute | solution.py:176
  15.6 14.1 %collective-permute-start.2 = (bf16[4,144,256]{2,1,0:T(8,128)(2,1)}, bf16[4,144,256]{2,1,0:T(8,128)(2,1)}, u32[]{:S(2)}, u32[]{:S(2)}) collective-permute-start(bf16[4,144,256]{2,1,0:T(8,128)(2,1)} %get-tuple-element.142), channel_id=1, source_target_pairs={{0,3},{1,2},{2,1},{3,0},{4,7},{5,6},{6,5},{7,4},{8,11},{9,10},{10,... | collective-permute-start | bytes 884744 | tf_op jit(solution)/shard_map/ppermute | solution.py:176
  31.8 26.1 %collective-permute-start.3 = (bf16[2,576,256]{2,1,0:T(8,128)(2,1)}, bf16[2,576,256]{2,1,0:T(8,128)(2,1)}, u32[]{:S(2)}, u32[]{:S(2)}) collective-permute-start(bf16[2,576,256]{2,1,0:T(8,128)(2,1)} %get-tuple-element.140), channel_id=1, source_target_pairs={{0,4},{4,8},{8,12},{1,5},{5,9},{9,13},{2,6},{6,10},{10,14},{3,7},{... | collective-permute-start | bytes 1769480 | tf_op jit(solution)/shard_map/ppermute | solution.py:22
  36.0 21.8 %collective-permute-start.4 = (bf16[2,576,256]{2,1,0:T(8,128)(2,1)}, bf16[2,576,256]{2,1,0:T(8,128)(2,1)}, u32[]{:S(2)}, u32[]{:S(2)}) collective-permute-start(bf16[2,576,256]{2,1,0:T(8,128)(2,1)} %get-tuple-element.141), channel_id=1, source_target_pairs={{4,0},{8,4},{12,8},{5,1},{9,5},{13,9},{6,2},{10,6},{14,10},{7,3},{... | collective-permute-start | bytes 1769480 | tf_op jit(solution)/shard_map/ppermute | solution.py:25
  283.2 23.0 %copy-start.7 = (f32[256,2,4]{2,1,0:T(2,128)S(1)}, f32[256,2,4]{2,1,0:T(2,128)}, u32[]{:S(2)}) copy-start(f32[256,2,4]{2,1,0:T(2,128)} %copy.34) | copy-start | bytes 24580
  306.2 3.8 copy-start.5
  306.2 3.8 copy-start.6
  306.2 3.8 copy-start.8
  306.2 3.8 copy-start.9
  306.2 5.8 %copy-start.3 = (bf16[2048,128]{1,0:T(8,128)(2,1)S(1)}, bf16[2048,128]{1,0:T(8,128)(2,1)}, u32[]{:S(2)}) copy-start(bf16[2048,128]{1,0:T(8,128)(2,1)} %gather_fusion.4) | copy-start | bytes 1572868
  306.3 5.8 %copy-start.4 = (bf16[2048,128]{1,0:T(8,128)(2,1)S(1)}, bf16[2048,128]{1,0:T(8,128)(2,1)}, u32[]{:S(2)}) copy-start(bf16[2048,128]{1,0:T(8,128)(2,1)} %gather_fusion.5) | copy-start | bytes 1572868
  306.3 5.8 %copy-start.10 = (f32[256,2,4]{2,1,0:T(2,128)S(1)}, f32[256,2,4]{2,1,0:T(2,128)}, u32[]{:S(2)}) copy-start(f32[256,2,4]{2,1,0:T(2,128)} %copy.44) | copy-start | bytes 24580
  306.3 5.8 %copy-start.11 = (f32[256,2,4]{2,1,0:T(2,128)S(1)}, f32[256,2,4]{2,1,0:T(2,128)}, u32[]{:S(2)}) copy-start(f32[256,2,4]{2,1,0:T(2,128)} %copy.42) | copy-start | bytes 24580
  310.0 4.0 copy-start.12
  310.0 4.0 copy-start.13
  314.1 2.4 copy-start.16
  316.1 40.7 %copy-start.2 = (bf16[256,1024]{1,0:T(8,128)(2,1)S(1)}, bf16[256,1024]{1,0:T(8,128)(2,1)}, u32[]{:S(2)}) copy-start(bf16[256,1024]{1,0:T(8,128)(2,1)} %param.19) | copy-start | bytes 1572868
  317.9 47.4 %copy-start.20 = (f32[896]{0:T(1024)S(1)}, f32[896]{0:T(1024)}, u32[]{:S(2)}) copy-start(f32[896]{0:T(1024)} %param.29) | copy-start | bytes 10756
  317.9 69.8 %all-gather.2.cloned.1.call-start = ((), (), s32[]{:S(2)}) async-start(), calls=%async_computation.1 | async-start | bytes 2293760 | tf_op jit(solution)/shard_map/all_gather | solution.py:203
  390.6 8.1 %copy-start.24 = (f32[768]{0:T(1024)S(1)}, f32[768]{0:T(1024)}, u32[]{:S(2)}) copy-start(f32[768]{0:T(1024)} %param.31) | copy-start | bytes 9220
  449.4 6.3 %copy-start.14 = (f32[6,256,128]{2,1,0:T(8,128)S(1)}, f32[6,256,128]{2,1,0:T(8,128)}, u32[]{:S(2)}) copy-start(f32[6,256,128]{2,1,0:T(8,128)} %get-tuple-element.260) | copy-start | bytes 2359300 | tf_op jit(solution)/shard_map/while
  452.9 2.8 copy-start.1
  461.2 6.3 %copy-start.14 = (f32[6,256,128]{2,1,0:T(8,128)S(1)}, f32[6,256,128]{2,1,0:T(8,128)}, u32[]{:S(2)}) copy-start(f32[6,256,128]{2,1,0:T(8,128)} %get-tuple-element.260) | copy-start | bytes 2359300 | tf_op jit(solution)/shard_map/while
  464.7 2.8 copy-start.1
  (3 other events, 3.4 us)
Sparse Core Ops, SparseCore 0:
  318.0 38.7 all-reduce.1
  366.4 21.2 all-gather.1
